TPU v7x, 32 devices: a 4x4x1 block of a 4x4x8 slice. The times are simulated.
32 devices in a mesh: data: 1 (over z), outer: 4 (over y), dap: 8 (over x, core).
Axes of the slice: x: 4, y: 4, z: 1, core: 2. Of those that a mesh axis runs over, the one named last changes fastest.
The devices are a block of a 4x4x8 slice.
Arguments:
- msa_rep: bfloat16 [256, 128, 256], P('data', ('outer', 'dap'))
- msa_mask: int32 [256, 128], P('data')
- pair_rep: float32 [128, 128, 128], P(('data', 'outer', 'dap'))
- ln_gamma: bfloat16 [256], replicated
- ln_beta: bfloat16 [256], replicated
- w_left: bfloat16 [256, 32], replicated
- b_left: bfloat16 [32], replicated
- w_right: bfloat16 [256, 32], replicated
- b_right: bfloat16 [32], replicated
- w_out: bfloat16 [1024, 128], replicated
- b_out: bfloat16 [128], replicated
Outputs:
- output 1: float32 [128, 128, 128], P(('data', 'outer', 'dap'))
- output 2: bfloat16 [256, 128, 256], P(('data', 'outer', 'dap'))
All inputs are finite; a program needn't handle non-finite values.
Results may differ from a plain program's by a relative error of at most 0.00395037.
Values are sent between devices in bfloat16 or wider.
A program may use at most 768 MiB of HBM per device.

v0:
```python
import functools

import jax
import jax.numpy as jnp
from jax import lax
from jax.experimental import pallas as pl
from jax.experimental.pallas import tpu as pltpu
from jax.sharding import PartitionSpec as P

LN_EPS = 1e-5
NORM_EPS = 1e-3
MESH = pl.DeviceIdType.MESH
F32 = jnp.float32
BF16 = jnp.bfloat16
LN_CHUNKS = 4
EARLY_AT = 0
EARLY = 0
MIDDLE = 31


def kernel(
    n_y, n_dap,
    m_hbm, mask_hbm, z_hbm, gamma_hbm, beta_hbm, wl_hbm, bl_hbm, wr_hbm, br_hbm, wo_hbm, bo_hbm,
    pair_ref, msa_ref,
    m_v, mask_v, gamma_v, beta_v, wl_v, bl_v, wr_v, br_v, wo_v, bo_v,
    m_got, y_s, a_all, b_col, o_s, w_s, w_perm, lhs_s, den_s, r_send, r_got,
    in_sem, m_sem, own_sem, m_send, m_recv,
    a_send, a_recv, b_send, b_recv, p_send, p_recv, r_ssem, r_rsem,
):
    n_x = n_dap // 2
    n_dev = n_y * n_dap
    n_seq, rows, chans = m_v.shape
    seq_own = n_seq // n_dev
    opm = wl_v.shape[0]
    n_res = mask_v.shape[1]
    group = 2 * rows
    line = n_y * group
    y = lax.axis_index("outer")
    d = lax.axis_index("dap")
    x, c = d // 2, d % 2
    me = y * n_dap + d

    def dev(dy, dx, dc):
        return {"outer": (y + dy) % n_y, "dap": ((x + dx) % n_x) * 2 + (c + dc) % 2}

    def remote(src, dst, send, recv, where):
        return pltpu.make_async_remote_copy(
            src_ref=src, dst_ref=dst, send_sem=send, recv_sem=recv, device_id=where, device_id_type=MESH
        )

    def wait_in(ref, sem):
        remote(ref, ref, sem, sem, dev(0, 0, 1)).wait_recv()

    sends = []

    def go(copy):
        copy.start()
        sends.append(copy)

    order_x = [1, n_x - 1] + list(range(2, n_x - 1))
    order_y = [1, n_y - 1] + list(range(2, n_y - 1))
    offsets = [(dy, dx, dc) for dx in range(n_x) for dy in range(n_y) for dc in range(2) if dy or dx or dc]

    piece = n_seq // LN_CHUNKS
    m_in = []
    for k in range(LN_CHUNKS):
        part = pl.ds(k * piece, piece)
        m_in.append(pltpu.make_async_copy(m_hbm.at[part], m_v.at[part], m_sem.at[k]))
    pairs = [
        (gamma_hbm, gamma_v), (beta_hbm, beta_v), (wl_hbm, wl_v), (wr_hbm, wr_v), (bl_hbm, bl_v), (br_hbm, br_v),
        (mask_hbm, mask_v), (wo_hbm, wo_v), (bo_hbm, bo_v), (z_hbm, pair_ref),
    ]
    small_in = [pltpu.make_async_copy(src, dst, in_sem.at[i]) for i, (src, dst) in enumerate(pairs)]
    for copy in small_in[:2] + m_in[:1] + small_in[2:6] + m_in[1:] + small_in[6:]:
        copy.start()
    barrier = pltpu.get_barrier_semaphore()
    for off in offsets:
        pl.semaphore_signal(barrier, inc=1, device_id=dev(*off), device_id_type=MESH)

    m_copies = []
    for i, off in enumerate(offsets):
        to = dev(*off)
        p = to["outer"] * n_dap + to["dap"]
        m_copies.append(
            remote(m_v.at[pl.ds(p * seq_own, seq_own)], m_got.at[:, me], m_send.at[i], m_recv.at[i], to)
        )

    for copy in small_in[:6]:
        copy.wait()
    w_both = jnp.concatenate([wl_v[...], wr_v[...]], axis=0)
    b_both = jnp.concatenate([bl_v[...].astype(F32), br_v[...].astype(F32)]).reshape(1, 2 * opm)
    gamma = gamma_v[...].astype(F32).reshape(1, chans)
    beta = beta_v[...].astype(F32).reshape(1, chans)

    def normalise(k):
        if k < EARLY_AT or not EARLY:
            m_in[k].wait()
        v = m_v[k * piece:(k + 1) * piece].astype(F32).reshape(piece * rows, chans)
        mean = jnp.mean(v, axis=-1, keepdims=True)
        cen = v - mean
        var = jnp.mean(cen * cen, axis=-1, keepdims=True)
        xn = (cen * lax.rsqrt(var + LN_EPS) * gamma + beta).astype(BF16)
        out = lax.dot_general(xn, w_both, (((1,), (1,)), ((), ())), preferred_element_type=F32) + b_both
        y_s[k * piece * rows:(k + 1) * piece * rows, :] = out

    for k in range(EARLY_AT):
        normalise(k)
    if EARLY:
        for k in range(EARLY_AT, LN_CHUNKS):
            m_in[k].wait()
        pl.semaphore_wait(barrier, n_dev - 1)
        for copy in m_copies[:EARLY]:
            go(copy)


    for k in range(EARLY_AT, LN_CHUNKS):
        normalise(k)

    small_in[6].wait()
    mask_b = mask_v[...].astype(F32).astype(BF16)
    row_of = lax.broadcasted_iota(jnp.int32, (n_res, rows * opm), 0)
    col_of = lax.broadcasted_iota(jnp.int32, (n_res, rows * opm), 1)
    pick = jnp.where(row_of == me * rows + col_of // opm, 1.0, 0.0).astype(BF16)
    mask_own = jnp.dot(mask_b, pick, preferred_element_type=F32)

    ys = [y_s[pl.ds(r, n_seq, stride=rows), :] for r in range(rows)]
    a_all[0] = (jnp.concatenate([t[:, :opm] for t in ys], axis=1) * mask_own).astype(BF16)
    b_own = jnp.concatenate([t[:, opm:] for t in ys], axis=1) * mask_own
    b_col[y * 2 + c] = b_own.T.astype(BF16)

    if not EARLY:
        pl.semaphore_wait(barrier, n_dev - 1)

    mine = b_col.at[y * 2 + c]
    go(remote(mine, mine, p_send.at[0], p_recv.at[0], dev(0, 0, 1)))
    for k in order_y:
        go(remote(mine, mine, b_send.at[k], b_recv.at[k], dev(k, 0, 0)))
    for k in order_x:
        go(remote(a_all.at[0], a_all.at[k], a_send.at[k], a_recv.at[k], dev(0, k, 0)))
    keep = pltpu.make_async_copy(m_v.at[pl.ds(me * seq_own, seq_own)], m_got.at[:, me], own_sem)
    keep.start()
    for copy in m_copies[EARLY:MIDDLE]:
        go(copy)

    for copy in small_in[7:]:
        copy.wait()
    w_s[...] = wo_v[...].astype(F32)
    for e in range(opm):
        w_perm[e * opm:(e + 1) * opm, :] = w_s[pl.ds(e, opm, stride=opm), :].astype(BF16)
    count = lax.dot_general(
        mask_b, mask_own.astype(BF16), (((0,), (0,)), ((), ())), preferred_element_type=F32
    )
    for i in range(rows):
        den_s[i] = jnp.broadcast_to(NORM_EPS + count[:, i * opm:i * opm + 1], den_s.shape[1:])
    bias_out = bo_v[...].astype(F32).reshape(1, -1)

    for k in order_y:
        got = b_col.at[((y + n_y - k) % n_y) * 2 + c]
        wait_in(got, b_recv.at[k])
        go(remote(got, got, p_send.at[k], p_recv.at[k], dev(0, 0, 1)))
    for k in range(n_y):
        wait_in(mine, p_recv.at[k])

    per = 128 // opm

    def outer(k):
        b_line = b_col[...].reshape(line * opm, n_seq)
        o_s[...] = jnp.dot(b_line, a_all[k], preferred_element_type=F32)
        for g in range(opm // per):
            parts = [o_s[pl.ds(g * per + q, line, stride=opm), :] for q in range(per)]
            for i in range(rows):
                block = jnp.concatenate([t[:, i * opm:(i + 1) * opm] for t in parts], axis=1)
                lhs_s[i * line:(i + 1) * line, g * 128:(g + 1) * 128] = block.astype(BF16)
        return jnp.dot(lhs_s[...], w_perm[...], preferred_element_type=F32)

    def finish(res, xs):
        for i in range(rows):
            for t in range(n_y):
                at = pl.ds(pl.multiple_of(t * n_x * group + xs * group, group), group)
                part = res[(i * n_y + t) * group:(i * n_y + t + 1) * group]
                pair_ref[i, at, :] += (part + bias_out) / den_s[i, at, :]

    for k in order_x[2:] + order_x[:2]:
        wait_in(a_all.at[k], a_recv.at[k])
        r_send[k] = outer(k)
        go(remote(r_send.at[k], r_got.at[k], r_ssem.at[k], r_rsem.at[k], dev(0, n_x - k, 0)))
    for copy in m_copies[MIDDLE:]:
        go(copy)
    finish(outer(0), x)
    for k in order_x[2:] + order_x[:2]:
        wait_in(r_got.at[k], r_rsem.at[k])
        finish(r_got[k], (x + k) % n_x)

    for copy in m_copies:
        copy.wait_recv()
    keep.wait()
    for s in range(seq_own):
        msa_ref[s] = m_got[s].astype(F32).reshape(n_res, chans).astype(BF16)
    for copy in sends:
        copy.wait_send()


def solution(mesh):
    n_y, n_dap = mesh.shape["outer"], mesh.shape["dap"]
    n_x, n_dev = n_dap // 2, n_y * n_dap
    dap_axes = ("outer", "dap")
    group_axes = ("data", "outer", "dap")

    def local_step(msa, mask, pair, gamma, beta, w_left, b_left, w_right, b_right, w_out, b_out):
        n_seq, rows, chans = msa.shape
        n_res = mask.shape[1]
        opm = w_left.shape[1]
        pair_dim = w_out.shape[1]
        seq_own = n_seq // n_dev
        line = n_y * 2 * rows
        dma = pltpu.SemaphoreType.DMA
        vmem = pl.BlockSpec(memory_space=pltpu.VMEM)
        ins = (msa, mask, pair, gamma, beta, w_left.T, b_left, w_right.T, b_right, w_out, b_out)
        return pl.pallas_call(
            functools.partial(kernel, n_y, n_dap),
            out_shape=(
                pltpu.VMEM(pair.shape, F32),
                pltpu.VMEM((seq_own, n_dev * rows, chans), BF16),
            ),
            in_specs=[pl.BlockSpec(memory_space=pl.ANY)] * len(ins),
            out_specs=(vmem, vmem),
            scratch_shapes=[pltpu.VMEM(v.shape, v.dtype) for v in ins[:2] + ins[3:]] + [
                pltpu.VMEM((seq_own, n_dev, rows, chans), BF16),
                pltpu.VMEM((n_seq * rows, 2 * opm), F32),
                pltpu.VMEM((n_x, n_seq, rows * opm), BF16),
                pltpu.VMEM((n_y * 2, rows * opm, n_seq), BF16),
                pltpu.VMEM((line * opm, rows * opm), F32),
                pltpu.VMEM((opm * opm, pair_dim), F32),
                pltpu.VMEM((opm * opm, pair_dim), BF16),
                pltpu.VMEM((rows * line, opm * opm), BF16),
                pltpu.VMEM((rows, n_res, pair_dim), F32),
                pltpu.VMEM((n_x, rows * line, pair_dim), F32),
                pltpu.VMEM((n_x, rows * line, pair_dim), F32),
                dma((10,)), dma((LN_CHUNKS,)), dma, dma((n_dev - 1,)), dma((n_dev - 1,)),
                dma((n_x,)), dma((n_x,)), dma((n_y,)), dma((n_y,)), dma((n_y,)), dma((n_y,)), dma((n_x,)), dma((n_x,)),
            ],
            compiler_params=pltpu.CompilerParams(collective_id=0, has_side_effects=True),
        )(*ins)

    return jax.shard_map(
        local_step, mesh=mesh,
        in_specs=(P("data", dap_axes, None), P("data", None), P(group_axes, None, None)) + (P(),) * 8,
        out_specs=(P(group_axes, None, None), P(group_axes, None, None)), check_vma=False,
    )
```

profile of v0, /device:TPU:97, one launch (start us, length us, event | category | flops | bytes accessed | tf_op | source)
XLA Modules:
  0.0 27.1 jit_solution(12023444806484765935)
XLA Ops:
  0.6 25.0 %shard_map.122 = (f32[4,128,128]{2,1,0:T(8,128)S(1)}, bf16[8,128,256]{2,1,0:T(8,128)(2,1)S(1)}) custom-call(bf16[256,4,256]{2,1,0:T(4,128)(2,1)} %m_hbm.1, s32[256,128]{1,0:T(8,128)} %mask_hbm.1, f32[4,128,128]{2,1,0:T(8,128)} %z_hbm.1, bf16[256]{0:T(256)(128)(2,1)} %gamma_hbm.1, bf16[256]{0:T(256)(128)(2,1)} %beta_hbm.1, bf16[32,256]{1,0:T(8,128)(2,1)} %bitcast.2, ...), custom_call_target="tpu_custom_call" | custom-call | tf_op jit(solution)/shard_map/pallas_call | solution.py:219
  25.6 0.7 %copy.15 = f32[4,128,128]{2,1,0:T(8,128)} copy(f32[4,128,128]{2,1,0:T(8,128)S(1)} %get-tuple-element.2) | data formatting | bytes 524288
  26.3 0.8 %copy.16 = bf16[8,128,256]{2,1,0:T(8,128)(2,1)} copy(bf16[8,128,256]{2,1,0:T(8,128)(2,1)S(1)} %get-tuple-element.3) | data formatting | bytes 1048576
where the time goes:
time: 27.2 us; the launch traced here: 27.1 us
  Pallas kernels  25 us (92%)
  local copies, waits for them, and re-layouts  1.5 us (6%)
  between operations  0.64 us (2%)
    pallas_call x1, Pallas kernels, local_step(): pl.pallas_call(functools.partial(kernel, n_y, n_dap), out_shape=(pltpu.VM...  25 us
    unnamed x2, local copies, waits for them, and re-layouts  1.5 us

commit v1 on v0

--- a/solution.py
+++ b/solution.py
@@ -12,10 +12,9 @@
 MESH = pl.DeviceIdType.MESH
 F32 = jnp.float32
 BF16 = jnp.bfloat16
-LN_CHUNKS = 4
-EARLY_AT = 0
-EARLY = 0
-MIDDLE = 31
+LN_CHUNKS = 1
+M_FIRST = 0
+M_STEPS = (31, 0, 0)
 
 
 def kernel(
@@ -23,7 +22,7 @@
     m_hbm, mask_hbm, z_hbm, gamma_hbm, beta_hbm, wl_hbm, bl_hbm, wr_hbm, br_hbm, wo_hbm, bo_hbm,
     pair_ref, msa_ref,
     m_v, mask_v, gamma_v, beta_v, wl_v, bl_v, wr_v, br_v, wo_v, bo_v,
-    m_got, y_s, a_all, b_col, o_s, w_s, w_perm, lhs_s, den_s, r_send, r_got,
+    m_got, y_s, a_all, b_row, o_s, w_s, w_perm, lhs_s, den_s, r_send, r_got,
     in_sem, m_sem, own_sem, m_send, m_recv,
     a_send, a_recv, b_send, b_recv, p_send, p_recv, r_ssem, r_rsem,
 ):
@@ -33,8 +32,7 @@
     seq_own = n_seq // n_dev
     opm = wl_v.shape[0]
     n_res = mask_v.shape[1]
-    group = 2 * rows
-    line = n_y * group
+    line = n_dap * rows
     y = lax.axis_index("outer")
     d = lax.axis_index("dap")
     x, c = d // 2, d % 2
@@ -57,9 +55,11 @@
         copy.start()
         sends.append(copy)
 
-    order_x = [1, n_x - 1] + list(range(2, n_x - 1))
-    order_y = [1, n_y - 1] + list(range(2, n_y - 1))
+    order_x = list(range(2, n_x - 1)) + [1, n_x - 1]
+    order_y = list(range(2, n_y - 1)) + [1, n_y - 1]
     offsets = [(dy, dx, dc) for dx in range(n_x) for dy in range(n_y) for dc in range(2) if dy or dx or dc]
+
+    offsets.sort(key=lambda o: -(min(o[0], n_y - o[0]) + min(o[1], n_x - o[1])))
 
     piece = n_seq // LN_CHUNKS
     m_in = []
@@ -82,7 +82,7 @@
         to = dev(*off)
         p = to["outer"] * n_dap + to["dap"]
         m_copies.append(
-            remote(m_v.at[pl.ds(p * seq_own, seq_own)], m_got.at[:, me], m_send.at[i], m_recv.at[i], to)
+            remote(m_v.at[pl.ds(p * seq_own, seq_own)], m_got.at[me], m_send.at[i], m_recv.at[i], to)
         )
 
     for copy in small_in[:6]:
@@ -93,8 +93,7 @@
     beta = beta_v[...].astype(F32).reshape(1, chans)
 
     def normalise(k):
-        if k < EARLY_AT or not EARLY:
-            m_in[k].wait()
+        m_in[k].wait()
         v = m_v[k * piece:(k + 1) * piece].astype(F32).reshape(piece * rows, chans)
         mean = jnp.mean(v, axis=-1, keepdims=True)
         cen = v - mean
@@ -103,17 +102,7 @@
         out = lax.dot_general(xn, w_both, (((1,), (1,)), ((), ())), preferred_element_type=F32) + b_both
         y_s[k * piece * rows:(k + 1) * piece * rows, :] = out
 
-    for k in range(EARLY_AT):
-        normalise(k)
-    if EARLY:
-        for k in range(EARLY_AT, LN_CHUNKS):
-            m_in[k].wait()
-        pl.semaphore_wait(barrier, n_dev - 1)
-        for copy in m_copies[:EARLY]:
-            go(copy)
-
-
-    for k in range(EARLY_AT, LN_CHUNKS):
+    for k in range(LN_CHUNKS):
         normalise(k)
 
     small_in[6].wait()
@@ -126,21 +115,24 @@
     ys = [y_s[pl.ds(r, n_seq, stride=rows), :] for r in range(rows)]
     a_all[0] = (jnp.concatenate([t[:, :opm] for t in ys], axis=1) * mask_own).astype(BF16)
     b_own = jnp.concatenate([t[:, opm:] for t in ys], axis=1) * mask_own
-    b_col[y * 2 + c] = b_own.T.astype(BF16)
-
-    if not EARLY:
-        pl.semaphore_wait(barrier, n_dev - 1)
-
-    mine = b_col.at[y * 2 + c]
+    b_row[d] = b_own.T.astype(BF16)
+
+    left = list(m_copies)
+
+    def send_m(count):
+        for _ in range(min(count, len(left))):
+            go(left.pop(0))
+
+    pl.semaphore_wait(barrier, n_dev - 1)
+    send_m(M_FIRST)
+    mine = b_row.at[d]
     go(remote(mine, mine, p_send.at[0], p_recv.at[0], dev(0, 0, 1)))
-    for k in order_y:
-        go(remote(mine, mine, b_send.at[k], b_recv.at[k], dev(k, 0, 0)))
-    for k in order_x:
-        go(remote(a_all.at[0], a_all.at[k], a_send.at[k], a_recv.at[k], dev(0, k, 0)))
-    keep = pltpu.make_async_copy(m_v.at[pl.ds(me * seq_own, seq_own)], m_got.at[:, me], own_sem)
+    for kx, ky in zip(order_x, order_y, strict=True):
+        go(remote(mine, mine, b_send.at[kx], b_recv.at[kx], dev(0, kx, 0)))
+        go(remote(a_all.at[0], a_all.at[ky], a_send.at[ky], a_recv.at[ky], dev(ky, 0, 0)))
+    keep = pltpu.make_async_copy(m_v.at[pl.ds(me * seq_own, seq_own)], m_got.at[me], own_sem)
     keep.start()
-    for copy in m_copies[EARLY:MIDDLE]:
-        go(copy)
+    send_m(M_STEPS[0])
 
     for copy in small_in[7:]:
         copy.wait()
@@ -154,17 +146,18 @@
         den_s[i] = jnp.broadcast_to(NORM_EPS + count[:, i * opm:i * opm + 1], den_s.shape[1:])
     bias_out = bo_v[...].astype(F32).reshape(1, -1)
 
-    for k in order_y:
-        got = b_col.at[((y + n_y - k) % n_y) * 2 + c]
+    for k in order_x:
+        got = b_row.at[((x + n_x - k) % n_x) * 2 + c]
         wait_in(got, b_recv.at[k])
         go(remote(got, got, p_send.at[k], p_recv.at[k], dev(0, 0, 1)))
-    for k in range(n_y):
+    send_m(M_STEPS[1])
+    for k in range(n_x):
         wait_in(mine, p_recv.at[k])
 
     per = 128 // opm
 
     def outer(k):
-        b_line = b_col[...].reshape(line * opm, n_seq)
+        b_line = b_row[...].reshape(line * opm, n_seq)
         o_s[...] = jnp.dot(b_line, a_all[k], preferred_element_type=F32)
         for g in range(opm // per):
             parts = [o_s[pl.ds(g * per + q, line, stride=opm), :] for q in range(per)]
@@ -173,31 +166,37 @@
                 lhs_s[i * line:(i + 1) * line, g * 128:(g + 1) * 128] = block.astype(BF16)
         return jnp.dot(lhs_s[...], w_perm[...], preferred_element_type=F32)
 
-    def finish(res, xs):
+    def finish(res, ys):
+        at = pl.ds(pl.multiple_of(ys * line, line), line)
         for i in range(rows):
-            for t in range(n_y):
-                at = pl.ds(pl.multiple_of(t * n_x * group + xs * group, group), group)
-                part = res[(i * n_y + t) * group:(i * n_y + t + 1) * group]
-                pair_ref[i, at, :] += (part + bias_out) / den_s[i, at, :]
-
-    for k in order_x[2:] + order_x[:2]:
+            pair_ref[i, at, :] += (res[i * line:(i + 1) * line] + bias_out) / den_s[i, at, :]
+
+    for k in order_y:
         wait_in(a_all.at[k], a_recv.at[k])
         r_send[k] = outer(k)
-        go(remote(r_send.at[k], r_got.at[k], r_ssem.at[k], r_rsem.at[k], dev(0, n_x - k, 0)))
-    for copy in m_copies[MIDDLE:]:
-        go(copy)
-    finish(outer(0), x)
-    for k in order_x[2:] + order_x[:2]:
+        go(remote(r_send.at[k], r_got.at[k], r_ssem.at[k], r_rsem.at[k], dev(n_y - k, 0, 0)))
+    send_m(M_STEPS[2])
+    finish(outer(0), y)
+    send_m(len(left))
+    for k in order_y:
         wait_in(r_got.at[k], r_rsem.at[k])
-        finish(r_got[k], (x + k) % n_x)
+        finish(r_got[k], (y + k) % n_y)
 
     for copy in m_copies:
         copy.wait_recv()
     keep.wait()
     for s in range(seq_own):
-        msa_ref[s] = m_got[s].astype(F32).reshape(n_res, chans).astype(BF16)
+        msa_ref[s] = m_got[:, s].astype(F32).reshape(n_res, chans).astype(BF16)
     for copy in sends:
         copy.wait_send()
+
+
+def store(pair_v, msa_v, pair_ref, msa_ref, sem):
+    copies = [pltpu.make_async_copy(pair_v, pair_ref, sem.at[0]), pltpu.make_async_copy(msa_v, msa_ref, sem.at[1])]
+    for copy in copies:
+        copy.start()
+    for copy in copies:
+        copy.wait()
 
 
 def solution(mesh):
@@ -212,11 +211,11 @@
         opm = w_left.shape[1]
         pair_dim = w_out.shape[1]
         seq_own = n_seq // n_dev
-        line = n_y * 2 * rows
+        line = n_dap * rows
         dma = pltpu.SemaphoreType.DMA
         vmem = pl.BlockSpec(memory_space=pltpu.VMEM)
         ins = (msa, mask, pair, gamma, beta, w_left.T, b_left, w_right.T, b_right, w_out, b_out)
-        return pl.pallas_call(
+        got = pl.pallas_call(
             functools.partial(kernel, n_y, n_dap),
             out_shape=(
                 pltpu.VMEM(pair.shape, F32),
@@ -225,22 +224,30 @@
             in_specs=[pl.BlockSpec(memory_space=pl.ANY)] * len(ins),
             out_specs=(vmem, vmem),
             scratch_shapes=[pltpu.VMEM(v.shape, v.dtype) for v in ins[:2] + ins[3:]] + [
-                pltpu.VMEM((seq_own, n_dev, rows, chans), BF16),
+                pltpu.VMEM((n_dev, seq_own, rows, chans), BF16),
                 pltpu.VMEM((n_seq * rows, 2 * opm), F32),
-                pltpu.VMEM((n_x, n_seq, rows * opm), BF16),
-                pltpu.VMEM((n_y * 2, rows * opm, n_seq), BF16),
+                pltpu.VMEM((n_y, n_seq, rows * opm), BF16),
+                pltpu.VMEM((n_dap, rows * opm, n_seq), BF16),
                 pltpu.VMEM((line * opm, rows * opm), F32),
                 pltpu.VMEM((opm * opm, pair_dim), F32),
                 pltpu.VMEM((opm * opm, pair_dim), BF16),
                 pltpu.VMEM((rows * line, opm * opm), BF16),
                 pltpu.VMEM((rows, n_res, pair_dim), F32),
-                pltpu.VMEM((n_x, rows * line, pair_dim), F32),
-                pltpu.VMEM((n_x, rows * line, pair_dim), F32),
+                pltpu.VMEM((n_y, rows * line, pair_dim), F32),
+                pltpu.VMEM((n_y, rows * line, pair_dim), F32),
                 dma((10,)), dma((LN_CHUNKS,)), dma, dma((n_dev - 1,)), dma((n_dev - 1,)),
-                dma((n_x,)), dma((n_x,)), dma((n_y,)), dma((n_y,)), dma((n_y,)), dma((n_y,)), dma((n_x,)), dma((n_x,)),
+                dma((n_y,)), dma((n_y,)), dma((n_x,)), dma((n_x,)), dma((n_x,)), dma((n_x,)), dma((n_y,)), dma((n_y,)),
             ],
             compiler_params=pltpu.CompilerParams(collective_id=0, has_side_effects=True),
         )(*ins)
+        return pl.pallas_call(
+            store,
+            out_shape=tuple(jax.ShapeDtypeStruct(v.shape, v.dtype) for v in got),
+            in_specs=[pl.BlockSpec(memory_space=pl.ANY)] * 2,
+            out_specs=(pl.BlockSpec(memory_space=pl.ANY),) * 2,
+            scratch_shapes=[dma((2,))],
+            compiler_params=pltpu.CompilerParams(vmem_limit_bytes=4 * 1024 * 1024),
+        )(*got)
 
     return jax.shard_map(
         local_step, mesh=mesh,

time: 27.2 us -> 24.3 us (0.89)
  Pallas kernels: 25 us -> 23.5 us
  local copies, waits for them, and re-layouts: 1.5 us -> 0 us
    pallas_call x1, Pallas kernels: 25 us -> 22.6 us  [local_step(): pl.pallas_call(functools.partial(kernel, n_y, n_dap), out_shape=(pltpu.VM...]
    unnamed x2 -> x0, local copies, waits for them, and re-layouts: 1.5 us -> none
    pallas_call x0 -> x1, Pallas kernels: none -> 0.9 us  [local_step(): pl.pallas_call(store, out_shape=tuple((jax.ShapeDtypeStruct(v.shape, v.dt...]
where the time goes in v1:
time: 24.3 us; the launch traced here: 24.2 us
  Pallas kernels  23.5 us (97%)
  between operations  0.64 us (3%)
    pallas_call x1, Pallas kernels, local_step(): pl.pallas_call(functools.partial(kernel, n_y, n_dap), out_shape=(pltpu.VM...  22.6 us
    pallas_call x1, Pallas kernels, local_step(): pl.pallas_call(store, out_shape=tuple((jax.ShapeDtypeStruct(v.shape, v.dt...  0.9 us

profile of v1, /device:TPU:97, one launch (start us, length us, event | category | flops | bytes accessed | tf_op | source)
XLA Modules:
  0.0 24.2 jit_solution(17232819107574490322)
XLA Ops:
  0.6 22.6 %shard_map.122 = (f32[4,128,128]{2,1,0:T(8,128)S(1)}, bf16[8,128,256]{2,1,0:T(8,128)(2,1)S(1)}) custom-call(bf16[256,4,256]{2,1,0:T(4,128)(2,1)} %m_hbm.1, s32[256,128]{1,0:T(8,128)} %mask_hbm.1, f32[4,128,128]{2,1,0:T(8,128)} %z_hbm.1, bf16[256]{0:T(256)(128)(2,1)} %gamma_hbm.1, bf16[256]{0:T(256)(128)(2,1)} %beta_hbm.1, bf16[32,256]{1,0:T(8,128)(2,1)} %bitcast.2, ...), custom_call_target="tpu_custom_call" | custom-call | tf_op jit(solution)/shard_map/pallas_call | solution.py:218
  23.3 0.9 %shard_map.123 = (f32[4,128,128]{2,1,0:T(8,128)}, bf16[8,128,256]{2,1,0:T(8,128)(2,1)}) custom-call(f32[4,128,128]{2,1,0:T(8,128)S(1)} %get-tuple-element.4.pair_v, bf16[8,128,256]{2,1,0:T(8,128)(2,1)S(1)} %get-tuple-element.5.msa_v), custom_call_target="tpu_custom_call" | custom-call | tf_op jit(solution)/shard_map/pallas_call | solution.py:243

commit v2 on v1

--- a/solution.py
+++ b/solution.py
@@ -32,14 +32,18 @@
     seq_own = n_seq // n_dev
     opm = wl_v.shape[0]
     n_res = mask_v.shape[1]
-    line = n_dap * rows
+    line = n_x * rows
     y = lax.axis_index("outer")
     d = lax.axis_index("dap")
     x, c = d // 2, d % 2
     me = y * n_dap + d
 
+    ys = [lax.rem(y + k, n_y) for k in range(n_y)]
+    xs = [lax.rem(x + k, n_x) for k in range(n_x)]
+    cs = [c, 1 - c]
+
     def dev(dy, dx, dc):
-        return {"outer": (y + dy) % n_y, "dap": ((x + dx) % n_x) * 2 + (c + dc) % 2}
+        return {"outer": ys[dy % n_y], "dap": xs[dx % n_x] * 2 + cs[dc]}
 
     def remote(src, dst, send, recv, where):
         return pltpu.make_async_remote_copy(
@@ -59,7 +63,7 @@
     order_y = list(range(2, n_y - 1)) + [1, n_y - 1]
     offsets = [(dy, dx, dc) for dx in range(n_x) for dy in range(n_y) for dc in range(2) if dy or dx or dc]
 
-    offsets.sort(key=lambda o: -(min(o[0], n_y - o[0]) + min(o[1], n_x - o[1])))
+    offsets.sort(key=lambda o: (-o[2], -(min(o[0], n_y - o[0]) + min(o[1], n_x - o[1]))))
 
     piece = n_seq // LN_CHUNKS
     m_in = []
@@ -112,10 +116,10 @@
     pick = jnp.where(row_of == me * rows + col_of // opm, 1.0, 0.0).astype(BF16)
     mask_own = jnp.dot(mask_b, pick, preferred_element_type=F32)
 
-    ys = [y_s[pl.ds(r, n_seq, stride=rows), :] for r in range(rows)]
-    a_all[0] = (jnp.concatenate([t[:, :opm] for t in ys], axis=1) * mask_own).astype(BF16)
-    b_own = jnp.concatenate([t[:, opm:] for t in ys], axis=1) * mask_own
-    b_row[d] = b_own.T.astype(BF16)
+    proj = [y_s[pl.ds(r, n_seq, stride=rows), :] for r in range(rows)]
+    a_all[0] = (jnp.concatenate([t[:, :opm] for t in proj], axis=1) * mask_own).astype(BF16)
+    b_own = jnp.concatenate([t[:, opm:] for t in proj], axis=1) * mask_own
+    b_row[x] = b_own.T.astype(BF16)
 
     left = list(m_copies)
 
@@ -125,8 +129,8 @@
 
     pl.semaphore_wait(barrier, n_dev - 1)
     send_m(M_FIRST)
-    mine = b_row.at[d]
-    go(remote(mine, mine, p_send.at[0], p_recv.at[0], dev(0, 0, 1)))
+    mine = b_row.at[x]
+    go(remote(mine, b_row.at[n_x + x], p_send.at[0], p_recv.at[0], dev(0, 0, 1)))
     for kx, ky in zip(order_x, order_y, strict=True):
         go(remote(mine, mine, b_send.at[kx], b_recv.at[kx], dev(0, kx, 0)))
         go(remote(a_all.at[0], a_all.at[ky], a_send.at[ky], a_recv.at[ky], dev(ky, 0, 0)))
@@ -147,40 +151,62 @@
     bias_out = bo_v[...].astype(F32).reshape(1, -1)
 
     for k in order_x:
-        got = b_row.at[((x + n_x - k) % n_x) * 2 + c]
+        at = xs[n_x - k]
+        got = b_row.at[at]
         wait_in(got, b_recv.at[k])
-        go(remote(got, got, p_send.at[k], p_recv.at[k], dev(0, 0, 1)))
+        go(remote(got, b_row.at[n_x + at], p_send.at[k], p_recv.at[k], dev(0, 0, 1)))
     send_m(M_STEPS[1])
-    for k in range(n_x):
-        wait_in(mine, p_recv.at[k])
 
     per = 128 // opm
 
-    def outer(k):
-        b_line = b_row[...].reshape(line * opm, n_seq)
-        o_s[...] = jnp.dot(b_line, a_all[k], preferred_element_type=F32)
+    def outer(h, slots):
+        b_line = b_row[h * n_x:(h + 1) * n_x].reshape(line * opm, n_seq)
+        a_pair = jnp.concatenate([a_all[k] for k in slots], axis=1)
+        both = jnp.dot(b_line, a_pair, preferred_element_type=F32)
+        for t in range(len(slots)):
+            o_s[t] = both[:, t * rows * opm:(t + 1) * rows * opm]
         for g in range(opm // per):
-            parts = [o_s[pl.ds(g * per + q, line, stride=opm), :] for q in range(per)]
-            for i in range(rows):
-                block = jnp.concatenate([t[:, i * opm:(i + 1) * opm] for t in parts], axis=1)
-                lhs_s[i * line:(i + 1) * line, g * 128:(g + 1) * 128] = block.astype(BF16)
-        return jnp.dot(lhs_s[...], w_perm[...], preferred_element_type=F32)
-
-    def finish(res, ys):
-        at = pl.ds(pl.multiple_of(ys * line, line), line)
+            for t in range(len(slots)):
+                parts = [o_s[t, pl.ds(g * per + q, line, stride=opm), :].astype(BF16) for q in range(per)]
+                for i in range(rows):
+                    block = jnp.concatenate([v[:, i * opm:(i + 1) * opm] for v in parts], axis=1)
+                    to = (t * rows + i) * line
+                    lhs_s[to:to + line, g * 128:(g + 1) * 128] = block.astype(BF16)
+        res = jnp.dot(lhs_s[...], w_perm[...], preferred_element_type=F32)
+        return [res[t * rows * line:(t + 1) * rows * line] for t in range(len(slots))]
+
+    def finish(h, res, row):
         for i in range(rows):
-            pair_ref[i, at, :] += (res[i * line:(i + 1) * line] + bias_out) / den_s[i, at, :]
-
-    for k in order_y:
-        wait_in(a_all.at[k], a_recv.at[k])
-        r_send[k] = outer(k)
-        go(remote(r_send.at[k], r_got.at[k], r_ssem.at[k], r_rsem.at[k], dev(n_y - k, 0, 0)))
-    send_m(M_STEPS[2])
-    finish(outer(0), y)
+            for t in range(n_x):
+                at = pl.ds((row * n_x + t) * 2 * rows + cs[h] * rows, rows)
+                part = res[(i * n_x + t) * rows:(i * n_x + t + 1) * rows]
+                pair_ref[i, at, :] += (part + bias_out) / den_s[i, at, :]
+
+    slots = order_y + [0]
+    own = []
+    for h in range(2):
+        if h == 1:
+            for k in range(n_x):
+                wait_in(mine, p_recv.at[k])
+        for n in range(0, n_y, 2):
+            pick_two = slots[n:n + 2]
+            if h == 0:
+                for k in pick_two:
+                    if k:
+                        wait_in(a_all.at[k], a_recv.at[k])
+            for k, res in zip(pick_two, outer(h, pick_two), strict=True):
+                r_send[k, h] = res
+                if k:
+                    go(remote(
+                        r_send.at[k, h], r_got.at[k, h], r_ssem.at[k, h], r_rsem.at[k, h], dev(n_y - k, 0, 0)
+                    ))
+            send_m(M_STEPS[2])
     send_m(len(left))
-    for k in order_y:
-        wait_in(r_got.at[k], r_rsem.at[k])
-        finish(r_got[k], (y + k) % n_y)
+    for h in range(2):
+        finish(h, r_send[0, h], y)
+        for k in order_y:
+            wait_in(r_got.at[k, h], r_rsem.at[k, h])
+            finish(h, r_got[k, h], ys[k])
 
     for copy in m_copies:
         copy.wait_recv()
@@ -211,7 +237,7 @@
         opm = w_left.shape[1]
         pair_dim = w_out.shape[1]
         seq_own = n_seq // n_dev
-        line = n_dap * rows
+        line = n_x * rows
         dma = pltpu.SemaphoreType.DMA
         vmem = pl.BlockSpec(memory_space=pltpu.VMEM)
         ins = (msa, mask, pair, gamma, beta, w_left.T, b_left, w_right.T, b_right, w_out, b_out)
@@ -228,15 +254,15 @@
                 pltpu.VMEM((n_seq * rows, 2 * opm), F32),
                 pltpu.VMEM((n_y, n_seq, rows * opm), BF16),
                 pltpu.VMEM((n_dap, rows * opm, n_seq), BF16),
-                pltpu.VMEM((line * opm, rows * opm), F32),
+                pltpu.VMEM((2, line * opm, rows * opm), F32),
                 pltpu.VMEM((opm * opm, pair_dim), F32),
                 pltpu.VMEM((opm * opm, pair_dim), BF16),
-                pltpu.VMEM((rows * line, opm * opm), BF16),
+                pltpu.VMEM((2 * rows * line, opm * opm), BF16),
                 pltpu.VMEM((rows, n_res, pair_dim), F32),
-                pltpu.VMEM((n_y, rows * line, pair_dim), F32),
-                pltpu.VMEM((n_y, rows * line, pair_dim), F32),
+                pltpu.VMEM((n_y, 2, rows * line, pair_dim), F32),
+                pltpu.VMEM((n_y, 2, rows * line, pair_dim), F32),
                 dma((10,)), dma((LN_CHUNKS,)), dma, dma((n_dev - 1,)), dma((n_dev - 1,)),
-                dma((n_y,)), dma((n_y,)), dma((n_x,)), dma((n_x,)), dma((n_x,)), dma((n_x,)), dma((n_y,)), dma((n_y,)),
+                dma((n_y,)), dma((n_y,)), dma((n_x,)), dma((n_x,)), dma((n_x,)), dma((n_x,)), dma((n_y, 2)), dma((n_y, 2)),
             ],
             compiler_params=pltpu.CompilerParams(collective_id=0, has_side_effects=True),
         )(*ins)

time: 24.3 us -> 23.9 us (0.984)
  Pallas kernels: 23.5 us -> 23 us
    pallas_call x1, Pallas kernels: 22.6 us -> 22.1 us  [local_step(): pl.pallas_call(functools.partial(kernel, n_y, n_dap), out_shape=(pltpu.VM...]
where the time goes in v2:
time: 23.9 us; the launch traced here: 23.7 us
  Pallas kernels  23 us (96%)
  between operations  0.64 us (3%)
    pallas_call x1, Pallas kernels, local_step(): pl.pallas_call(functools.partial(kernel, n_y, n_dap), out_shape=(pltpu.VM...  22.1 us
    pallas_call x1, Pallas kernels, local_step(): pl.pallas_call(store, out_shape=tuple((jax.ShapeDtypeStruct(v.shape, v.dt...  0.9 us

profile of v2, /device:TPU:97, one launch (start us, length us, event | category | flops | bytes accessed | tf_op | source)
XLA Modules:
  0.0 23.7 jit_solution(2959351041939906772)
XLA Ops:
  0.6 22.1 %shard_map.122 = (f32[4,128,128]{2,1,0:T(8,128)S(1)}, bf16[8,128,256]{2,1,0:T(8,128)(2,1)S(1)}) custom-call(bf16[256,4,256]{2,1,0:T(4,128)(2,1)} %m_hbm.1, s32[256,128]{1,0:T(8,128)} %mask_hbm.1, f32[4,128,128]{2,1,0:T(8,128)} %z_hbm.1, bf16[256]{0:T(256)(128)(2,1)} %gamma_hbm.1, bf16[256]{0:T(256)(128)(2,1)} %beta_hbm.1, bf16[32,256]{1,0:T(8,128)(2,1)} %bitcast.2, ...), custom_call_target="tpu_custom_call" | custom-call | tf_op jit(solution)/shard_map/pallas_call | solution.py:244
  22.8 0.9 %shard_map.123 = (f32[4,128,128]{2,1,0:T(8,128)}, bf16[8,128,256]{2,1,0:T(8,128)(2,1)}) custom-call(f32[4,128,128]{2,1,0:T(8,128)S(1)} %get-tuple-element.4.pair_v, bf16[8,128,256]{2,1,0:T(8,128)(2,1)S(1)} %get-tuple-element.5.msa_v), custom_call_target="tpu_custom_call" | custom-call | tf_op jit(solution)/shard_map/pallas_call | solution.py:269

commit v3 on v2

--- a/solution.py
+++ b/solution.py
@@ -13,6 +13,7 @@
 F32 = jnp.float32
 BF16 = jnp.bfloat16
 LN_CHUNKS = 1
+
 M_FIRST = 0
 M_STEPS = (31, 0, 0)
 
@@ -53,12 +54,6 @@
     def wait_in(ref, sem):
         remote(ref, ref, sem, sem, dev(0, 0, 1)).wait_recv()
 
-    sends = []
-
-    def go(copy):
-        copy.start()
-        sends.append(copy)
-
     order_x = list(range(2, n_x - 1)) + [1, n_x - 1]
     order_y = list(range(2, n_y - 1)) + [1, n_y - 1]
     offsets = [(dy, dx, dc) for dx in range(n_x) for dy in range(n_y) for dc in range(2) if dy or dx or dc]
@@ -75,7 +70,7 @@
         (mask_hbm, mask_v), (wo_hbm, wo_v), (bo_hbm, bo_v), (z_hbm, pair_ref),
     ]
     small_in = [pltpu.make_async_copy(src, dst, in_sem.at[i]) for i, (src, dst) in enumerate(pairs)]
-    for copy in small_in[:2] + m_in[:1] + small_in[2:6] + m_in[1:] + small_in[6:]:
+    for copy in small_in[6:7] + m_in + small_in[:6] + small_in[7:]:
         copy.start()
     barrier = pltpu.get_barrier_semaphore()
     for off in offsets:
@@ -86,8 +81,15 @@
         to = dev(*off)
         p = to["outer"] * n_dap + to["dap"]
         m_copies.append(
-            remote(m_v.at[pl.ds(p * seq_own, seq_own)], m_got.at[me], m_send.at[i], m_recv.at[i], to)
+            remote(m_v.at[pl.ds(p * seq_own, seq_own)], m_got.at[me], m_send, m_recv, to)
         )
+
+    small_in[6].wait()
+    mask_b = mask_v[...].astype(F32).astype(BF16)
+    row_of = lax.broadcasted_iota(jnp.int32, (n_res, rows * opm), 0)
+    col_of = lax.broadcasted_iota(jnp.int32, (n_res, rows * opm), 1)
+    pick = jnp.where(row_of == me * rows + col_of // opm, 1.0, 0.0).astype(BF16)
+    mask_own = jnp.dot(mask_b, pick, preferred_element_type=F32)
 
     for copy in small_in[:6]:
         copy.wait()
@@ -109,13 +111,6 @@
     for k in range(LN_CHUNKS):
         normalise(k)
 
-    small_in[6].wait()
-    mask_b = mask_v[...].astype(F32).astype(BF16)
-    row_of = lax.broadcasted_iota(jnp.int32, (n_res, rows * opm), 0)
-    col_of = lax.broadcasted_iota(jnp.int32, (n_res, rows * opm), 1)
-    pick = jnp.where(row_of == me * rows + col_of // opm, 1.0, 0.0).astype(BF16)
-    mask_own = jnp.dot(mask_b, pick, preferred_element_type=F32)
-
     proj = [y_s[pl.ds(r, n_seq, stride=rows), :] for r in range(rows)]
     a_all[0] = (jnp.concatenate([t[:, :opm] for t in proj], axis=1) * mask_own).astype(BF16)
     b_own = jnp.concatenate([t[:, opm:] for t in proj], axis=1) * mask_own
@@ -125,15 +120,15 @@
 
     def send_m(count):
         for _ in range(min(count, len(left))):
-            go(left.pop(0))
+            left.pop(0).start()
 
     pl.semaphore_wait(barrier, n_dev - 1)
     send_m(M_FIRST)
     mine = b_row.at[x]
-    go(remote(mine, b_row.at[n_x + x], p_send.at[0], p_recv.at[0], dev(0, 0, 1)))
+    remote(mine, b_row.at[n_x + x], p_send, p_recv.at[0], dev(0, 0, 1)).start()
     for kx, ky in zip(order_x, order_y, strict=True):
-        go(remote(mine, mine, b_send.at[kx], b_recv.at[kx], dev(0, kx, 0)))
-        go(remote(a_all.at[0], a_all.at[ky], a_send.at[ky], a_recv.at[ky], dev(ky, 0, 0)))
+        remote(mine, mine, b_send, b_recv.at[kx], dev(0, kx, 0)).start()
+        remote(a_all.at[0], a_all.at[ky], a_send, a_recv.at[ky], dev(ky, 0, 0)).start()
     keep = pltpu.make_async_copy(m_v.at[pl.ds(me * seq_own, seq_own)], m_got.at[me], own_sem)
     keep.start()
     send_m(M_STEPS[0])
@@ -154,7 +149,7 @@
         at = xs[n_x - k]
         got = b_row.at[at]
         wait_in(got, b_recv.at[k])
-        go(remote(got, b_row.at[n_x + at], p_send.at[k], p_recv.at[k], dev(0, 0, 1)))
+        remote(got, b_row.at[n_x + at], p_send, p_recv.at[0], dev(0, 0, 1)).start()
     send_m(M_STEPS[1])
 
     per = 128 // opm
@@ -172,7 +167,7 @@
                     block = jnp.concatenate([v[:, i * opm:(i + 1) * opm] for v in parts], axis=1)
                     to = (t * rows + i) * line
                     lhs_s[to:to + line, g * 128:(g + 1) * 128] = block.astype(BF16)
-        res = jnp.dot(lhs_s[...], w_perm[...], preferred_element_type=F32)
+        res = jnp.dot(lhs_s[:len(slots) * rows * line], w_perm[...], preferred_element_type=F32)
         return [res[t * rows * line:(t + 1) * rows * line] for t in range(len(slots))]
 
     def finish(h, res, row):
@@ -182,39 +177,34 @@
                 part = res[(i * n_x + t) * rows:(i * n_x + t + 1) * rows]
                 pair_ref[i, at, :] += (part + bias_out) / den_s[i, at, :]
 
-    slots = order_y + [0]
-    own = []
     for h in range(2):
         if h == 1:
-            for k in range(n_x):
-                wait_in(mine, p_recv.at[k])
-        for n in range(0, n_y, 2):
-            pick_two = slots[n:n + 2]
+            wait_in(b_row.at[pl.ds(n_x, n_x)], p_recv.at[0])
+        for slots in (order_y[:1], order_y[1:]):
             if h == 0:
-                for k in pick_two:
-                    if k:
-                        wait_in(a_all.at[k], a_recv.at[k])
-            for k, res in zip(pick_two, outer(h, pick_two), strict=True):
+                for k in slots:
+                    wait_in(a_all.at[k], a_recv.at[k])
+            for k, res in zip(slots, outer(h, slots), strict=True):
                 r_send[k, h] = res
-                if k:
-                    go(remote(
-                        r_send.at[k, h], r_got.at[k, h], r_ssem.at[k, h], r_rsem.at[k, h], dev(n_y - k, 0, 0)
-                    ))
-            send_m(M_STEPS[2])
+                remote(r_send.at[k, h], r_got.at[k, h], r_ssem, r_rsem.at[k, h], dev(n_y - k, 0, 0)).start()
     send_m(len(left))
     for h in range(2):
-        finish(h, r_send[0, h], y)
+        finish(h, outer(h, [0])[0], y)
+    for h in range(2):
         for k in order_y:
             wait_in(r_got.at[k, h], r_rsem.at[k, h])
             finish(h, r_got[k, h], ys[k])
 
-    for copy in m_copies:
-        copy.wait_recv()
+    arrived = m_got.at[pl.ds(0, n_dev - 1)]
+    wait_in(arrived, m_recv)
     keep.wait()
     for s in range(seq_own):
         msa_ref[s] = m_got[:, s].astype(F32).reshape(n_res, chans).astype(BF16)
-    for copy in sends:
-        copy.wait_send()
+    for ref, sem in [
+        (arrived, m_send), (a_all.at[pl.ds(0, n_y - 1)], a_send), (b_row.at[pl.ds(0, n_x - 1)], b_send),
+        (b_row.at[pl.ds(0, n_x)], p_send), (r_send.at[pl.ds(0, n_y - 1)], r_ssem),
+    ]:
+        remote(ref, ref, sem, sem, dev(0, 0, 1)).wait_send()
 
 
 def store(pair_v, msa_v, pair_ref, msa_ref, sem):
@@ -261,8 +251,8 @@
                 pltpu.VMEM((rows, n_res, pair_dim), F32),
                 pltpu.VMEM((n_y, 2, rows * line, pair_dim), F32),
                 pltpu.VMEM((n_y, 2, rows * line, pair_dim), F32),
-                dma((10,)), dma((LN_CHUNKS,)), dma, dma((n_dev - 1,)), dma((n_dev - 1,)),
-                dma((n_y,)), dma((n_y,)), dma((n_x,)), dma((n_x,)), dma((n_x,)), dma((n_x,)), dma((n_y, 2)), dma((n_y, 2)),
+                dma((10,)), dma((LN_CHUNKS,)), dma, dma, dma,
+                dma, dma((n_y,)), dma, dma((n_x,)), dma, dma((1,)), dma, dma((n_y, 2)),
             ],
             compiler_params=pltpu.CompilerParams(collective_id=0, has_side_effects=True),
         )(*ins)

time: 23.9 us -> 22.9 us (0.958)
  Pallas kernels: 23 us -> 22.1 us
    pallas_call x1, Pallas kernels: 22.1 us -> 21.2 us  [local_step(): pl.pallas_call(functools.partial(kernel, n_y, n_dap), out_shape=(pltpu.VM...]
where the time goes in v3:
time: 22.9 us; the launch traced here: 22.8 us
  Pallas kernels  22.1 us (97%)
  between operations  0.64 us (3%)
    pallas_call x1, Pallas kernels, local_step(): pl.pallas_call(functools.partial(kernel, n_y, n_dap), out_shape=(pltpu.VM...  21.2 us
    pallas_call x1, Pallas kernels, local_step(): pl.pallas_call(store, out_shape=tuple((jax.ShapeDtypeStruct(v.shape, v.dt...  0.9 us

profile of v3, /device:TPU:97, one launch (start us, length us, event | category | flops | bytes accessed | tf_op | source)
XLA Modules:
  0.0 22.8 jit_solution(17699867348910588298)
XLA Ops:
  0.6 21.2 %shard_map.122 = (f32[4,128,128]{2,1,0:T(8,128)S(1)}, bf16[8,128,256]{2,1,0:T(8,128)(2,1)S(1)}) custom-call(bf16[256,4,256]{2,1,0:T(4,128)(2,1)} %m_hbm.1, s32[256,128]{1,0:T(8,128)} %mask_hbm.1, f32[4,128,128]{2,1,0:T(8,128)} %z_hbm.1, bf16[256]{0:T(256)(128)(2,1)} %gamma_hbm.1, bf16[256]{0:T(256)(128)(2,1)} %beta_hbm.1, bf16[32,256]{1,0:T(8,128)(2,1)} %bitcast.2, ...), custom_call_target="tpu_custom_call" | custom-call | tf_op jit(solution)/shard_map/pallas_call | solution.py:234
  21.9 0.9 %shard_map.123 = (f32[4,128,128]{2,1,0:T(8,128)}, bf16[8,128,256]{2,1,0:T(8,128)(2,1)}) custom-call(f32[4,128,128]{2,1,0:T(8,128)S(1)} %get-tuple-element.4.pair_v, bf16[8,128,256]{2,1,0:T(8,128)(2,1)S(1)} %get-tuple-element.5.msa_v), custom_call_target="tpu_custom_call" | custom-call | tf_op jit(solution)/shard_map/pallas_call | solution.py:259

commit v4 on v3

--- a/solution.py
+++ b/solution.py
@@ -125,10 +125,10 @@
     pl.semaphore_wait(barrier, n_dev - 1)
     send_m(M_FIRST)
     mine = b_row.at[x]
-    remote(mine, b_row.at[n_x + x], p_send, p_recv.at[0], dev(0, 0, 1)).start()
     for kx, ky in zip(order_x, order_y, strict=True):
         remote(mine, mine, b_send, b_recv.at[kx], dev(0, kx, 0)).start()
         remote(a_all.at[0], a_all.at[ky], a_send, a_recv.at[ky], dev(ky, 0, 0)).start()
+    remote(mine, b_row.at[n_x + x], p_send, p_recv.at[0], dev(0, 0, 1)).start()
     keep = pltpu.make_async_copy(m_v.at[pl.ds(me * seq_own, seq_own)], m_got.at[me], own_sem)
     keep.start()
     send_m(M_STEPS[0])
@@ -190,16 +190,16 @@
     send_m(len(left))
     for h in range(2):
         finish(h, outer(h, [0])[0], y)
-    for h in range(2):
-        for k in order_y:
-            wait_in(r_got.at[k, h], r_rsem.at[k, h])
-            finish(h, r_got[k, h], ys[k])
-
     arrived = m_got.at[pl.ds(0, n_dev - 1)]
     wait_in(arrived, m_recv)
     keep.wait()
     for s in range(seq_own):
         msa_ref[s] = m_got[:, s].astype(F32).reshape(n_res, chans).astype(BF16)
+    for h in range(2):
+        for k in order_y:
+            wait_in(r_got.at[k, h], r_rsem.at[k, h])
+            finish(h, r_got[k, h], ys[k])
+
     for ref, sem in [
         (arrived, m_send), (a_all.at[pl.ds(0, n_y - 1)], a_send), (b_row.at[pl.ds(0, n_x - 1)], b_send),
         (b_row.at[pl.ds(0, n_x)], p_send), (r_send.at[pl.ds(0, n_y - 1)], r_ssem),

time: 22.9 us -> 22.5 us (0.983)
  Pallas kernels: 22.1 us -> 21.7 us
    pallas_call x1, Pallas kernels: 21.2 us -> 20.8 us  [local_step(): pl.pallas_call(functools.partial(kernel, n_y, n_dap), out_shape=(pltpu.VM...]
where the time goes in v4:
time: 22.5 us; the launch traced here: 22.3 us
  Pallas kernels  21.7 us (96%)
  between operations  0.64 us (3%)
    pallas_call x1, Pallas kernels, local_step(): pl.pallas_call(functools.partial(kernel, n_y, n_dap), out_shape=(pltpu.VM...  20.8 us
    pallas_call x1, Pallas kernels, local_step(): pl.pallas_call(store, out_shape=tuple((jax.ShapeDtypeStruct(v.shape, v.dt...  0.9 us

profile of v4, /device:TPU:97, one launch (start us, length us, event | category | flops | bytes accessed | tf_op | source)
XLA Modules:
  0.0 22.3 jit_solution(6301069329981018865)
XLA Ops:
  0.6 20.8 %shard_map.122 = (f32[4,128,128]{2,1,0:T(8,128)S(1)}, bf16[8,128,256]{2,1,0:T(8,128)(2,1)S(1)}) custom-call(bf16[256,4,256]{2,1,0:T(4,128)(2,1)} %m_hbm.1, s32[256,128]{1,0:T(8,128)} %mask_hbm.1, f32[4,128,128]{2,1,0:T(8,128)} %z_hbm.1, bf16[256]{0:T(256)(128)(2,1)} %gamma_hbm.1, bf16[256]{0:T(256)(128)(2,1)} %beta_hbm.1, bf16[32,256]{1,0:T(8,128)(2,1)} %bitcast.2, ...), custom_call_target="tpu_custom_call" | custom-call | tf_op jit(solution)/shard_map/pallas_call | solution.py:234
  21.4 0.9 %shard_map.123 = (f32[4,128,128]{2,1,0:T(8,128)}, bf16[8,128,256]{2,1,0:T(8,128)(2,1)}) custom-call(f32[4,128,128]{2,1,0:T(8,128)S(1)} %get-tuple-element.4.pair_v, bf16[8,128,256]{2,1,0:T(8,128)(2,1)S(1)} %get-tuple-element.5.msa_v), custom_call_target="tpu_custom_call" | custom-call | tf_op jit(solution)/shard_map/pallas_call | solution.py:259

commit v5 on v4

--- a/solution.py
+++ b/solution.py
@@ -142,7 +142,7 @@
         mask_b, mask_own.astype(BF16), (((0,), (0,)), ((), ())), preferred_element_type=F32
     )
     for i in range(rows):
-        den_s[i] = jnp.broadcast_to(NORM_EPS + count[:, i * opm:i * opm + 1], den_s.shape[1:])
+        den_s[i] = 1.0 / jnp.broadcast_to(NORM_EPS + count[:, i * opm:i * opm + 1], den_s.shape[1:])
     bias_out = bo_v[...].astype(F32).reshape(1, -1)
 
     for k in order_x:
@@ -175,7 +175,7 @@
             for t in range(n_x):
                 at = pl.ds((row * n_x + t) * 2 * rows + cs[h] * rows, rows)
                 part = res[(i * n_x + t) * rows:(i * n_x + t + 1) * rows]
-                pair_ref[i, at, :] += (part + bias_out) / den_s[i, at, :]
+                pair_ref[i, at, :] += (part + bias_out) * den_s[i, at, :]
 
     for h in range(2):
         if h == 1:

time: 22.5 us -> 22.4 us (level)
  no operation moved by 1% of the time
where the time goes in v5:
time: 22.4 us; the launch traced here: 22.3 us
  Pallas kernels  21.7 us (97%)
  between operations  0.64 us (3%)
    pallas_call x1, Pallas kernels, local_step(): pl.pallas_call(functools.partial(kernel, n_y, n_dap), out_shape=(pltpu.VM...  20.8 us
    pallas_call x1, Pallas kernels, local_step(): pl.pallas_call(store, out_shape=tuple((jax.ShapeDtypeStruct(v.shape, v.dt...  0.9 us

profile of v5, /device:TPU:97, one launch (start us, length us, event | category | flops | bytes accessed | tf_op | source)
XLA Modules:
  0.0 22.3 jit_solution(330277058728217749)
XLA Ops:
  0.6 20.8 %shard_map.122 = (f32[4,128,128]{2,1,0:T(8,128)S(1)}, bf16[8,128,256]{2,1,0:T(8,128)(2,1)S(1)}) custom-call(bf16[256,4,256]{2,1,0:T(4,128)(2,1)} %m_hbm.1, s32[256,128]{1,0:T(8,128)} %mask_hbm.1, f32[4,128,128]{2,1,0:T(8,128)} %z_hbm.1, bf16[256]{0:T(256)(128)(2,1)} %gamma_hbm.1, bf16[256]{0:T(256)(128)(2,1)} %beta_hbm.1, bf16[32,256]{1,0:T(8,128)(2,1)} %bitcast.2, ...), custom_call_target="tpu_custom_call" | custom-call | tf_op jit(solution)/shard_map/pallas_call | solution.py:234
  21.4 0.9 %shard_map.123 = (f32[4,128,128]{2,1,0:T(8,128)}, bf16[8,128,256]{2,1,0:T(8,128)(2,1)}) custom-call(f32[4,128,128]{2,1,0:T(8,128)S(1)} %get-tuple-element.4.pair_v, bf16[8,128,256]{2,1,0:T(8,128)(2,1)S(1)} %get-tuple-element.5.msa_v), custom_call_target="tpu_custom_call" | custom-call | tf_op jit(solution)/shard_map/pallas_call | solution.py:259
